TPU v7x, 256 devices: a 8x8x2 block of a 8x8x16 slice. The times are simulated.
256 devices in a mesh: grp: 2 (over z), kvp: 16 (over x, core), tp: 8 (over y).
Axes of the slice: x: 8, y: 8, z: 2, core: 2. Of those that a mesh axis runs over, the one named last changes fastest.
The devices are a block of a 8x8x16 slice.
Arguments:
- hidden_in: bfloat16 [16, 7168], P('grp'), parts along dimension 0, may hold values from -3 to 3
- queries_nope: bfloat16 [16, 128, 128], P('grp', ('kvp', 'tp')), parts along dimension 0, may hold values from -6 to 6
- queries_rope: bfloat16 [16, 128, 64], P('grp', ('kvp', 'tp')), parts along dimension 0, may hold values from -26 to 26
- cache: bfloat16 [16, 6144, 576], P('grp', 'kvp'), parts along dimension 0, may hold values from -20 to 20
- lengths: int32 [16], P('grp'), parts along dimension 0, may hold values from 128 to 6144, as said below
- w_uk: bfloat16 [128, 128, 512], P(('kvp', 'tp')), may hold values from -0.5 to 0.5
- w_uv: bfloat16 [128, 512, 128], P(('kvp', 'tp')), may hold values from -0.25 to 0.25
- w_out: bfloat16 [16384, 7168], P(('kvp', 'tp')), may hold values from -0.1875 to 0.1875
- norm_gain: float32 [7168], replicated, may hold values from 0.25 to 1.75
- w_gate: bfloat16 [7168, 18432], P(None, ('kvp', 'tp')), may hold values from -0.0625 to 0.0625
- w_up: bfloat16 [7168, 18432], P(None, ('kvp', 'tp')), may hold values from -0.0625 to 0.0625
- w_down: bfloat16 [18432, 7168], P(('kvp', 'tp')), may hold values from -0.15625 to 0.15625
Outputs:
- layer_out: bfloat16 [16, 7168], P('grp', ('kvp', 'tp')), parts along dimension 0
There are 2 independent parts, one for each index of `grp`. A program takes and returns all parts, laid end to end along the dimension named above; an argument that names none is the same for every part. Nothing has to cross between parts.
Inputs may be any that keep to these rules, and one draw needn't show every extreme that they name: `lengths`: every length is a multiple of 128; in every draw some request has the full 6144.
All inputs are finite; a program needn't handle non-finite values.
Results may differ from a plain program's by a relative error of at most 0.04.
Values may be sent and summed in bfloat16 or wider, within the bound.
A program may use at most 64 MiB of HBM per device.

v0:
```python
import jax
import jax.numpy as jnp
from jax import lax
from jax.sharding import Mesh
from jax.sharding import PartitionSpec as P

KVP = ("kvp_0", "kvp_1")
KVP_TP = ("kvp_0", "kvp_1", "tp")


def in_one_piece(arrays, axis, dim, along):
    both = jnp.concatenate(arrays, axis=along)
    whole, at, gathered = (lax.all_gather(both, axis, axis=dim, tiled=True), 0, [])
    for a in arrays:
        gathered.append(lax.slice_in_dim(whole, at, at + a.shape[along], axis=along))
        at += a.shape[along]
    return tuple(gathered)


def sum_in_order(blocks, axes, sequence):
    inside = blocks.shape[1:]
    blocks = blocks.reshape(*(lax.axis_size(a) for a in axes), *inside)
    blocks = jnp.moveaxis(blocks, sequence, range(len(axes))).reshape(-1, *inside)
    for k in sequence:
        blocks = lax.psum_scatter(blocks, axes[k], scatter_dimension=0, tiled=True)
    return blocks[0]


def in_blocks(value, dim, size):
    dims = value.shape
    blocks = value.reshape(*dims[:dim], size, dims[dim] // size, *dims[dim + 1 :])
    return jnp.moveaxis(blocks, dim, 0)


def sum_by_axis(value, axes, sequence, dim):
    size = lax.axis_size(axes)
    return sum_in_order(in_blocks(value, dim, size), axes, sequence)


def project(o_lat, w_uv, w_out):
    head_out = jnp.einsum("bhl,hle->bhe", o_lat, w_uv, preferred_element_type=jnp.float32).astype(
        jnp.bfloat16
    )
    return jnp.dot(
        head_out.reshape(head_out.shape[0], -1), w_out, preferred_element_type=jnp.float32
    )


def per_device(
    hidden_in,
    queries_nope,
    queries_rope,
    cache,
    lengths,
    w_uk,
    w_uv,
    w_out,
    norm_gain,
    w_gate,
    w_up,
    w_down,
):
    batch, heads_dev, head_dim = queries_nope.shape
    latent = w_uk.shape[2]
    ctx_dev = cache.shape[1]
    groups = lax.axis_size(KVP)
    score_scale = float(head_dim + queries_rope.shape[2]) ** (-0.5)
    q_lat = jnp.einsum(
        "bhd,hdl->bhl", queries_nope, w_uk, preferred_element_type=jnp.float32
    ).astype(jnp.bfloat16)
    q_lat_all, rope_all = in_one_piece((q_lat, queries_rope), KVP, 1, 2)
    q_full = jnp.concatenate([q_lat_all, rope_all], axis=2)
    scores = (
        jnp.einsum("bhc,btc->bht", q_full, cache, preferred_element_type=jnp.float32) * score_scale
    )
    offset = lax.axis_index(KVP) * ctx_dev
    visible = ((offset + jnp.arange(ctx_dev, dtype=jnp.int32))[None, :] < lengths[:, None])[
        :, None, :
    ]
    masked = jnp.where(visible, scores, jnp.float32(-1e30))
    block_max = jnp.max(masked, axis=2)
    exponent = jnp.where(visible, jnp.exp(masked - block_max[..., None]), jnp.float32(0.0))
    guarded = jnp.maximum(jnp.sum(exponent, axis=2), 1.0)
    log_total = block_max + jnp.log(guarded)
    weights = (exponent / guarded[..., None]).astype(jnp.bfloat16)
    partial_value = jnp.einsum("bht,btc->bhc", weights, cache, preferred_element_type=jnp.float32)[
        ..., :latent
    ]
    blocks = partial_value.reshape(batch, groups, heads_dev, latent)
    block_logs = log_total.reshape(batch, groups, heads_dev)
    part_blocks = lax.all_to_all(
        blocks.astype(jnp.bfloat16), KVP, split_axis=1, concat_axis=1, tiled=True
    ).astype(blocks.dtype)
    part_logs = lax.all_to_all(
        block_logs.astype(jnp.bfloat16), KVP, split_axis=1, concat_axis=1, tiled=True
    ).astype(block_logs.dtype)
    highest = jnp.max(part_logs, axis=1)
    overall = highest + jnp.log(jnp.sum(jnp.exp(part_logs - highest[:, None, :]), axis=1))
    scaled = jnp.exp(part_logs - overall[:, None, :])[..., None] * part_blocks
    o_lat = jnp.sum(scaled, axis=1).astype(jnp.bfloat16)
    attention = project(o_lat, w_uv, w_out)
    model_width = norm_gain.shape[0]
    share_width = model_width // lax.axis_size(KVP_TP)
    share_start = lax.axis_index(KVP_TP) * share_width
    attn_whole = lax.psum(attention, KVP_TP)
    residual = hidden_in.astype(jnp.float32) + attn_whole
    mean_square = jnp.mean(residual * residual, axis=1)
    normed = (residual * lax.rsqrt(mean_square + 1e-06)[:, None] * norm_gain[None, :]).astype(
        jnp.bfloat16
    )
    residual_share = lax.dynamic_slice_in_dim(residual, share_start, share_width, 1)
    gate_proj = jnp.dot(normed, w_gate, preferred_element_type=jnp.float32)
    up_proj = jnp.dot(normed, w_up, preferred_element_type=jnp.float32)
    act = (jax.nn.silu(gate_proj) * up_proj).astype(jnp.bfloat16)
    ffn_terms = jnp.dot(act, w_down, preferred_element_type=jnp.float32)
    ffn_share = sum_by_axis(ffn_terms, KVP_TP, (1, 0, 2), 1)
    return (residual_share + ffn_share).astype(jnp.bfloat16)


def solution(mesh):
    torus = Mesh(
        mesh.devices.reshape(mesh.shape["grp"], 8, 2, mesh.shape["tp"]),
        ("grp", "kvp_0", "kvp_1", "tp"),
    )
    return jax.shard_map(
        per_device,
        mesh=torus,
        in_specs=(
            P("grp", None),
            P("grp", KVP_TP, None),
            P("grp", KVP_TP, None),
            P("grp", KVP, None),
            P("grp"),
            P(KVP_TP, None, None),
            P(KVP_TP, None, None),
            P(KVP_TP, None),
            P(),
            P(None, KVP_TP),
            P(None, KVP_TP),
            P(KVP_TP, None),
        ),
        out_specs=P("grp", KVP_TP),
        check_vma=False,
    )
```

profile of v0, /device:TPU:514, one launch (start us, length us, event | category | flops | bytes accessed | tf_op | source)
XLA Modules:
  0.0 365.7 jit_solution(1368219524394948218)
XLA Ops:
  6.6 1.2 fusion.1
  7.7 0.7 pad_maximum_fusion
  8.4 34.0 %all_gather.3 = bf16[8,16,576]{2,0,1:T(8,128)(2,1)S(1)} all-gather(bf16[8,1,576]{2,0,1:T(8,128)(2,1)S(1)} %pad_maximum_fusion), channel_id=1, replica_groups=mesh['grp'=2,'kvp_0'=8,'kvp_1'=2,'tp'=8] {'kvp_0','kvp_1'}, dimensions={1}, use_global_device_ids=true | all-gather | bytes 156672 | tf_op jit(solution)/shard_map/all_gather | solution.py:13
  42.4 0.7 broadcast_compare_fusion
  43.1 0.7 fusion.35
  43.8 0.7 copy-done.2
  44.5 0.2 fusion.6
  44.7 0.6 fusion.30
  45.3 0.7 copy.24
  45.9 3.6 all-to-all-start
  49.5 2.0 fusion.11
  51.6 0.7 copy.27
  52.3 3.4 all-to-all-done
  55.7 5.4 %all-to-all-start.1 = ((bf16[8,16,1,512]{3,0,2,1:T(8,128)(2,1)}), bf16[8,16,1,512]{3,0,2,1:T(8,128)(2,1)}, u32[]{:S(2)}, u32[]{:S(2)}) async-start(bf16[8,16,1,512]{3,0,2,1:T(8,128)(2,1)} %copy.27), calls=%async_computation.1 | async-start | bytes 262144 | tf_op jit(solution)/shard_map/all_to_all | solution.py:91
  61.2 0.5 reduce_max.25
  61.7 0.1 copy.25
  61.8 0.8 fusion.24
  62.8 5.9 %all-to-all-done.1 = bf16[8,16,1,512]{3,0,2,1:T(8,128)(2,1)} async-done(((bf16[8,16,1,512]{3,0,2,1:T(8,128)(2,1)}), bf16[8,16,1,512]{3,0,2,1:T(8,128)(2,1)}, u32[]{:S(2)}, u32[]{:S(2)}) %all-to-all-start.1) | async-done | bytes 131104 | tf_op jit(solution)/shard_map/all_to_all | solution.py:91
  68.7 1.0 multiply_reduce_fusion
  69.7 2.7 fusion.4
  72.5 185.7 %all-reduce.3.cloned.1.call-done = f32[8,7168]{1,0:T(8,128)} async-done(((f32[8,7168]{1,0:T(8,128)}), f32[8,7168]{1,0:T(8,128)}) %all-reduce.3.cloned.1.call-update) | async-done | bytes 229392 | tf_op jit(solution)/shard_map/psum | solution.py:105
  258.3 1.2 multiply_reduce_fusion.1
  259.5 0.7 copy-done.1
  260.2 2.3 fusion.34
  262.4 4.6 %fusion.3 = f32[8,7168]{1,0:T(8,128)} fusion(bf16[144,7168]{1,0:T(8,128)(2,1)} %param.23, bf16[7168,144]{0,1:T(8,128)(2,1)} %param.22, f32[8,144]{1,0:T(8,128)S(1)} %fusion.34, f32[8,7168]{1,0:T(8,128)} %copy-done.1, f32[7168]{0:T(1024)} %param.20, f32[8]{0:T(128)S(1)} %add_rsqrt_fusion), kind=kOutput, calls=%fused_computation.6 | convolution fusion | flops 33209088 | bytes 4620832 | tf_op jit(solution)/shard_map/dot_general | solution.py:115
  267.1 2.2 reshape.125
  269.3 2.2 copy.29
  271.5 12.6 %reduce-scatter.3.cloned.1.call-done = f32[64,8,56]{2,1,0:T(8,128)} async-done(((f32[128,8,56]{2,1,0:T(8,128)}), f32[64,8,56]{2,1,0:T(8,128)}) %reduce-scatter.3.cloned.1.call-update) | async-done | bytes 114704 | tf_op jit(solution)/shard_map/reduce_scatter | solution.py:25
  284.3 0.6 dynamic-slice
  284.8 41.0 %reduce-scatter.5.cloned.1.call-done = f32[8,8,56]{2,1,0:T(8,128)} async-done(((f32[64,8,56]{2,1,0:T(8,128)}), f32[8,8,56]{2,1,0:T(8,128)}) %reduce-scatter.5.cloned.1.call-update) | async-done | bytes 14352 | tf_op jit(solution)/shard_map/reduce_scatter | solution.py:25
  325.8 31.4 %all-reduce = f32[8,8,56]{2,1,0:T(8,128)} all-reduce(f32[8,8,56]{2,1,0:T(8,128)} %reduce-scatter.5.cloned.1.call-done), channel_id=4, replica_groups=mesh['grp'=2,'kvp_0'=8,'kvp_1'=2,'tp'=8] {'tp'}, use_global_device_ids=true, to_apply=%region_9.10.clone | all-reduce | flops 3584 | bytes 28672
  357.3 1.9 fusion.28
  (19 shorter events, 0.6 us)
Async XLA Ops:
  6.5 36.6 %copy-start = (bf16[8,384,576]{1,2,0:T(8,128)(2,1)S(1)}, bf16[8,384,576]{1,2,0:T(8,128)(2,1)}, u32[]{:S(2)}) copy-start(bf16[8,384,576]{1,2,0:T(8,128)(2,1)} %param.15) | copy-start | bytes 10616836
  43.8 0.7 copy-start.2
  45.9 9.8 %all-to-all-start = ((bf16[8,16,1]{0,2,1:T(2,128)(2,1)}), bf16[8,16,1]{0,2,1:T(2,128)(2,1)S(1)}, u32[]{:S(2)}, u32[]{:S(2)}) async-start(bf16[8,16,1]{0,2,1:T(2,128)(2,1)} %copy.24), calls=%async_computation | async-start | bytes 16384 | tf_op jit(solution)/shard_map/all_to_all | solution.py:94
  55.7 12.9 %all-to-all-start.1 = ((bf16[8,16,1,512]{3,0,2,1:T(8,128)(2,1)}), bf16[8,16,1,512]{3,0,2,1:T(8,128)(2,1)}, u32[]{:S(2)}, u32[]{:S(2)}) async-start(bf16[8,16,1,512]{3,0,2,1:T(8,128)(2,1)} %copy.27), calls=%async_computation.1 | async-start | bytes 262144 | tf_op jit(solution)/shard_map/all_to_all | solution.py:91
  61.1 197.2 %all-reduce.3.cloned.1.call-start = ((), (), s32[]{:S(2)}) async-start(), calls=%async_computation.4 | async-start | bytes 458752 | tf_op jit(solution)/shard_map/psum | solution.py:105
  72.5 211.7 %reduce-scatter.3.cloned.1.call-start = ((), (), s32[]{:S(2)}) async-start(), calls=%async_computation.5 | async-start | bytes 786432 | tf_op jit(solution)/shard_map/reduce_scatter | solution.py:25
  259.5 0.7 copy-start.1
  267.1 17.2 %copy-start.3 = (u32[256]{0:T(256)S(1)}, u32[256]{0:T(256)}, u32[]{:S(2)}) copy-start(u32[256]{0:T(256)} %constant.55) | copy-start | bytes 3076
  271.5 54.4 %reduce-scatter.5.cloned.1.call-start = ((), (), s32[]{:S(2)}) async-start(), calls=%async_computation.6 | async-start | bytes 294912 | tf_op jit(solution)/shard_map/reduce_scatter | solution.py:25
Sparse Core Ops, SparseCore 0:
  72.6 185.6 all-reduce.2
  271.6 12.5 reduce-scatter.2
  286.7 39.0 reduce-scatter.4
where the time goes:
time: 366 us
  waiting for transfers between devices  249 us (68%)
  blocking collectives  65.4 us (18%)
  matrix products  13.5 us (4%)
  between operations  13.2 us (4%)
  starting transfers between devices  9.14 us (2%)
  local copies, waits for them, and re-layouts  7.86 us (2%)
  other arithmetic  7.76 us (2%)
    psum x1, waiting for transfers between devices, per_device(): attn_whole = lax.psum(attention, KVP_TP)  186 us
    reduce_scatter x2, waiting for transfers between devices, sum_in_order(): blocks = lax.psum_scatter(blocks, axes[k], scatter_dimension=0, tiled=True)  53.6 us
    all_gather x1, blocking collectives, in_one_piece(): lax.all_gather(both, axis, axis=dim, tiled=True)  34 us
    unnamed x1, blocking collectives  31.4 us
  transfers between devices with their start and end apart: 5, of which 5 were waited for; matrix products, arithmetic and copies ran while one was open for 1% of the time, Pallas kernels for 0%

commit v1 on v0

--- a/solution.py
+++ b/solution.py
@@ -102,7 +102,7 @@
     model_width = norm_gain.shape[0]
     share_width = model_width // lax.axis_size(KVP_TP)
     share_start = lax.axis_index(KVP_TP) * share_width
-    attn_whole = lax.psum(attention, KVP_TP)
+    attn_whole = lax.psum(lax.psum(attention, ("kvp_1", "tp")), "kvp_0")
     residual = hidden_in.astype(jnp.float32) + attn_whole
     mean_square = jnp.mean(residual * residual, axis=1)
     normed = (residual * lax.rsqrt(mean_square + 1e-06)[:, None] * norm_gain[None, :]).astype(

time: 366 us -> 370 us (1.011)
    psum x1 -> x2, waiting for transfers between devices: 186 us -> 188 us  [per_device(): attn_whole = lax.psum(lax.psum(attention, ('kvp_1', 'tp')), 'kvp_0')]
  transfers between devices with their start and end apart: 5 -> 6, of which waited for: 5 -> 6; matrix products, arithmetic and copies ran while one was open for 1% -> 1% of each run, Pallas kernels for 0% -> 0%
where the time goes in v1:
time: 370 us; the launch traced here: 369 us
  waiting for transfers between devices  252 us (68%)
  blocking collectives  65.4 us (18%)
  matrix products  13.5 us (4%)
  between operations  13.2 us (4%)
  starting transfers between devices  9.2 us (2%)
  local copies, waits for them, and re-layouts  7.86 us (2%)
  other arithmetic  7.76 us (2%)
    psum x2, waiting for transfers between devices, per_device(): attn_whole = lax.psum(lax.psum(attention, ('kvp_1', 'tp')), 'kvp_0')  188 us
    reduce_scatter x2, waiting for transfers between devices, sum_in_order(): blocks = lax.psum_scatter(blocks, axes[k], scatter_dimension=0, tiled=True)  54.4 us
    all_gather x1, blocking collectives, in_one_piece(): lax.all_gather(both, axis, axis=dim, tiled=True)  34 us
    unnamed x1, blocking collectives  31.4 us
  transfers between devices with their start and end apart: 6, of which 6 were waited for; matrix products, arithmetic and copies ran while one was open for 1% of the time, Pallas kernels for 0%

profile of v1, /device:TPU:514, one launch (start us, length us, event | category | flops | bytes accessed | tf_op | source)
XLA Modules:
  0.0 369.2 jit_solution(10061599098883369812)
XLA Ops:
  6.6 1.2 fusion.1
  7.7 0.7 pad_maximum_fusion
  8.4 34.0 %all_gather.3 = bf16[8,16,576]{2,0,1:T(8,128)(2,1)S(1)} all-gather(bf16[8,1,576]{2,0,1:T(8,128)(2,1)S(1)} %pad_maximum_fusion), channel_id=1, replica_groups=mesh['grp'=2,'kvp_0'=8,'kvp_1'=2,'tp'=8] {'kvp_0','kvp_1'}, dimensions={1}, use_global_device_ids=true | all-gather | bytes 156672 | tf_op jit(solution)/shard_map/all_gather | solution.py:13
  42.4 0.7 broadcast_compare_fusion
  43.1 0.7 fusion.35
  43.8 0.7 copy-done.2
  44.5 0.2 fusion.6
  44.7 0.6 fusion.30
  45.3 0.7 copy.24
  45.9 3.6 all-to-all-start
  49.5 2.0 fusion.11
  51.6 0.7 copy.27
  52.3 3.4 all-to-all-done
  55.7 5.4 %all-to-all-start.1 = ((bf16[8,16,1,512]{3,0,2,1:T(8,128)(2,1)}), bf16[8,16,1,512]{3,0,2,1:T(8,128)(2,1)}, u32[]{:S(2)}, u32[]{:S(2)}) async-start(bf16[8,16,1,512]{3,0,2,1:T(8,128)(2,1)} %copy.27), calls=%async_computation.1 | async-start | bytes 262144 | tf_op jit(solution)/shard_map/all_to_all | solution.py:91
  61.2 0.5 reduce_max.25
  61.8 0.8 fusion.24
  62.8 5.9 %all-to-all-done.1 = bf16[8,16,1,512]{3,0,2,1:T(8,128)(2,1)} async-done(((bf16[8,16,1,512]{3,0,2,1:T(8,128)(2,1)}), bf16[8,16,1,512]{3,0,2,1:T(8,128)(2,1)}, u32[]{:S(2)}, u32[]{:S(2)}) %all-to-all-start.1) | async-done | bytes 131104 | tf_op jit(solution)/shard_map/all_to_all | solution.py:91
  68.7 1.0 multiply_reduce_fusion
  69.7 2.7 fusion.4
  72.5 111.4 %all-reduce.4.cloned.1.call-done = f32[8,7168]{1,0:T(8,128)} async-done(((f32[8,7168]{1,0:T(8,128)}), f32[8,7168]{1,0:T(8,128)}) %all-reduce.4.cloned.1.call-update) | async-done | bytes 229392 | tf_op jit(solution)/shard_map/psum | solution.py:105
  184.0 77.0 %all-reduce.6.cloned.1.call-done = f32[8,7168]{1,0:T(8,128)} async-done(((f32[8,7168]{1,0:T(8,128)}), f32[8,7168]{1,0:T(8,128)}) %all-reduce.6.cloned.1.call-update) | async-done | bytes 229392 | tf_op jit(solution)/shard_map/psum | solution.py:105
  261.0 1.2 multiply_reduce_fusion.1
  262.2 0.7 copy-done.1
  262.9 2.3 fusion.34
  265.2 4.6 %fusion.3 = f32[8,7168]{1,0:T(8,128)} fusion(bf16[144,7168]{1,0:T(8,128)(2,1)} %param.23, bf16[7168,144]{0,1:T(8,128)(2,1)} %param.22, f32[8,144]{1,0:T(8,128)S(1)} %fusion.34, f32[8,7168]{1,0:T(8,128)} %copy-done.1, f32[7168]{0:T(1024)} %param.20, f32[8]{0:T(128)S(1)} %add_rsqrt_fusion), kind=kOutput, calls=%fused_computation.6 | convolution fusion | flops 33209088 | bytes 4620832 | tf_op jit(solution)/shard_map/dot_general | solution.py:115
  269.8 2.2 reshape.125
  272.0 2.2 copy.29
  274.3 13.6 %reduce-scatter.3.cloned.1.call-done = f32[64,8,56]{2,1,0:T(8,128)} async-done(((f32[128,8,56]{2,1,0:T(8,128)}), f32[64,8,56]{2,1,0:T(8,128)}) %reduce-scatter.3.cloned.1.call-update) | async-done | bytes 114704 | tf_op jit(solution)/shard_map/reduce_scatter | solution.py:25
  287.9 0.6 dynamic-slice
  288.5 40.8 %reduce-scatter.5.cloned.1.call-done = f32[8,8,56]{2,1,0:T(8,128)} async-done(((f32[64,8,56]{2,1,0:T(8,128)}), f32[8,8,56]{2,1,0:T(8,128)}) %reduce-scatter.5.cloned.1.call-update) | async-done | bytes 14352 | tf_op jit(solution)/shard_map/reduce_scatter | solution.py:25
  329.3 31.4 %all-reduce = f32[8,8,56]{2,1,0:T(8,128)} all-reduce(f32[8,8,56]{2,1,0:T(8,128)} %reduce-scatter.5.cloned.1.call-done), channel_id=4, replica_groups=mesh['grp'=2,'kvp_0'=8,'kvp_1'=2,'tp'=8] {'tp'}, use_global_device_ids=true, to_apply=%region_10.11.clone | all-reduce | flops 3584 | bytes 28672
  360.8 1.9 fusion.28
  (22 shorter events, 0.8 us)
Async XLA Ops:
  6.5 36.6 %copy-start = (bf16[8,384,576]{1,2,0:T(8,128)(2,1)S(1)}, bf16[8,384,576]{1,2,0:T(8,128)(2,1)}, u32[]{:S(2)}) copy-start(bf16[8,384,576]{1,2,0:T(8,128)(2,1)} %param.15) | copy-start | bytes 10616836
  43.8 0.7 copy-start.2
  45.9 9.8 %all-to-all-start = ((bf16[8,16,1]{0,2,1:T(2,128)(2,1)}), bf16[8,16,1]{0,2,1:T(2,128)(2,1)S(1)}, u32[]{:S(2)}, u32[]{:S(2)}) async-start(bf16[8,16,1]{0,2,1:T(2,128)(2,1)} %copy.24), calls=%async_computation | async-start | bytes 16384 | tf_op jit(solution)/shard_map/all_to_all | solution.py:94
  55.7 12.9 %all-to-all-start.1 = ((bf16[8,16,1,512]{3,0,2,1:T(8,128)(2,1)}), bf16[8,16,1,512]{3,0,2,1:T(8,128)(2,1)}, u32[]{:S(2)}, u32[]{:S(2)}) async-start(bf16[8,16,1,512]{3,0,2,1:T(8,128)(2,1)} %copy.27), calls=%async_computation.1 | async-start | bytes 262144 | tf_op jit(solution)/shard_map/all_to_all | solution.py:91
  61.1 122.8 %all-reduce.4.cloned.1.call-start = ((), (), s32[]{:S(2)}) async-start(), calls=%async_computation.4 | async-start | bytes 458752 | tf_op jit(solution)/shard_map/psum | solution.py:105
  72.5 188.5 %all-reduce.6.cloned.1.call-start = ((), (), s32[]{:S(2)}) async-start(), calls=%async_computation.5 | async-start | bytes 458752 | tf_op jit(solution)/shard_map/psum | solution.py:105
  184.0 103.9 %reduce-scatter.3.cloned.1.call-start = ((), (), s32[]{:S(2)}) async-start(), calls=%async_computation.6 | async-start | bytes 786432 | tf_op jit(solution)/shard_map/reduce_scatter | solution.py:25
  262.2 0.7 copy-start.1
  269.8 18.1 %copy-start.3 = (u32[256]{0:T(256)S(1)}, u32[256]{0:T(256)}, u32[]{:S(2)}) copy-start(u32[256]{0:T(256)} %constant.55) | copy-start | bytes 3076
  274.2 55.1 %reduce-scatter.5.cloned.1.call-start = ((), (), s32[]{:S(2)}) async-start(), calls=%async_computation.7 | async-start | bytes 294912 | tf_op jit(solution)/shard_map/reduce_scatter | solution.py:25
Sparse Core Ops, SparseCore 0:
  72.6 111.2 all-reduce.3
  186.3 74.6 all-reduce.5
  274.3 13.4 reduce-scatter.2
  290.2 39.0 reduce-scatter.4
